TPU v7x, 32 devices: a whole 2x2x4 slice. The times are simulated.
32 devices in a mesh: req: 8 (over z, core), blk: 4 (over y, x).
Axes of the slice: x: 2, y: 2, z: 4, core: 2. Of those that a mesh axis runs over, the one named last changes fastest.
Arguments:
- draft_node_queries: bfloat16 [256, 4096], P(('req', 'blk')), parts along dimension 0, may hold values from -6 to 6, as said below
- draft_node_keys: bfloat16 [256, 512], P(('req', 'blk')), parts along dimension 0, may hold values from -6 to 6
- draft_node_values: bfloat16 [256, 512], P(('req', 'blk')), parts along dimension 0, may hold values from -6 to 6
- paged_key_cache: bfloat16 [16384, 512], P(('req', 'blk')), parts along dimension 0, may hold values from -6 to 6
- paged_value_cache: bfloat16 [16384, 512], P(('req', 'blk')), parts along dimension 0, may hold values from -6 to 6
- context_length: int32 [8], P('req'), parts along dimension 0, may hold values from 1024 to 2048
- parents: int32 [256], P('req'), parts along dimension 0, may hold values from 0 to 31, as said below
- accepted_path: int32 [64], P('req'), parts along dimension 0, may hold values from 0 to 31, as said below
- out_weight: bfloat16 [2880, 4096], P('blk'), may hold values from -0.09375 to 0.09375
Outputs:
- tree_attention: bfloat16 [256, 4096], P(('req', 'blk')), parts along dimension 0
- path_output: bfloat16 [64, 2880], P('req', 'blk'), parts along dimension 0
There are 8 independent parts, one for each index of `req`. A program takes and returns all parts, laid end to end along the dimension named above; an argument that names none is the same for every part. Nothing has to cross between parts.
Inputs may be any that keep to these rules, and one draw needn't show every extreme that they name: `draft_node_queries`: query entries lie within the range. parents[0] = 0 marks the root; for i >= 1, parents[i] is one of the nodes i - 4 to i - 1 (and at least 0). `accepted_path`: distinct nodes; each entry after the first is a child of the one before it.
All inputs are finite; a program needn't handle non-finite values.
Results may differ from a plain program's by a relative error of at most 0.0095.
Values may be sent and summed in bfloat16 or wider, within the bound.
A program may use at most 64 MiB of HBM per device.

v0:
```python
import jax
import jax.numpy as jnp
from jax import lax
from jax.sharding import PartitionSpec as P

QUERY_HEADS = 64
KEY_VALUE_HEADS = 8
HEAD_WIDTH = 64
score_after_mask = -1e30


def ancestors(parents):
    draft_node_count = parents.shape[0]
    indices = jnp.arange(draft_node_count, dtype=jnp.int32)
    linked = (parents[:, None] == indices[None, :]) & (indices[:, None] > 0)
    ancestry = jnp.minimum(
        jnp.eye(draft_node_count, dtype=jnp.float32) + linked.astype(jnp.float32), 1.0
    )
    for squaring in range(7):
        ancestry = jnp.minimum(jnp.dot(ancestry, ancestry, precision=lax.Precision.HIGHEST), 1.0)
    return ancestry > 0.5


def fresh_state(cache_row_count):
    query_group_width = QUERY_HEADS // KEY_VALUE_HEADS
    return (
        jnp.full(
            (cache_row_count, KEY_VALUE_HEADS, query_group_width), score_after_mask, jnp.float32
        ),
        jnp.zeros((cache_row_count, KEY_VALUE_HEADS, query_group_width), jnp.float32),
        jnp.zeros((cache_row_count, KEY_VALUE_HEADS, query_group_width, HEAD_WIDTH), jnp.float32),
    )


def combine(first_part, second_part):
    maxima = jnp.maximum(first_part[0], second_part[0])
    first_scale = jnp.exp(first_part[0] - maxima)
    second_scale = jnp.exp(second_part[0] - maxima)
    totals = first_part[1] * first_scale + second_part[1] * second_scale
    weighted = first_part[2] * first_scale[..., None] + second_part[2] * second_scale[..., None]
    return (maxima, totals, weighted)


def fold_block(state, grouped_queries, flat_key_rows, flat_value_rows, usable):
    maxima, totals, weighted = state
    cache_row_count = flat_key_rows.shape[0]
    gathered_key_block = flat_key_rows.reshape(cache_row_count, KEY_VALUE_HEADS, HEAD_WIDTH)
    gathered_value_block = flat_value_rows.reshape(cache_row_count, KEY_VALUE_HEADS, HEAD_WIDTH)
    scores = jnp.einsum(
        "mrjz,xrz->mrjx", grouped_queries, gathered_key_block, preferred_element_type=jnp.float32
    ) * HEAD_WIDTH ** (-0.5)
    scores = jnp.where(usable, scores, score_after_mask)
    new_maxima = jnp.maximum(maxima, jnp.max(scores, axis=-1))
    weights = jnp.where(usable, jnp.exp(scores - new_maxima[..., None]), 0.0)
    rescale = jnp.exp(maxima - new_maxima)
    totals = totals * rescale + jnp.sum(weights, axis=-1)
    weighted = weighted * rescale[..., None] + jnp.einsum(
        "zvle,evt->zvlt",
        weights.astype(jnp.bfloat16),
        gathered_value_block,
        preferred_element_type=jnp.float32,
    )
    return (new_maxima, totals, weighted)


def cache_partial(grouped_queries, paged_key_cache, paged_value_cache, offset, length, state):
    rows_per_block = min(512, paged_key_cache.shape[0])
    block_table = paged_key_cache.shape[0] // rows_per_block
    gathered_key_blocks = paged_key_cache.reshape(
        block_table, rows_per_block, paged_key_cache.shape[1]
    )
    gathered_value_blocks = paged_value_cache.reshape(
        block_table, rows_per_block, paged_value_cache.shape[1]
    )
    starts = offset + rows_per_block * jnp.arange(block_table, dtype=jnp.int32)

    def step_fn(carried, pieces):
        usable = pieces[2] + jnp.arange(rows_per_block, dtype=jnp.int32) < length
        return (fold_block(carried, grouped_queries, pieces[0], pieces[1], usable), None)

    result, unused = lax.scan(step_fn, state, (gathered_key_blocks, gathered_value_blocks, starts))
    return result


def tree_partial(grouped_queries, keys_all, values_all, ancestry_rows):
    return fold_block(
        fresh_state(grouped_queries.shape[0]),
        grouped_queries,
        keys_all,
        values_all,
        ancestry_rows[:, None, None, :],
    )


def normalize(partial_value):
    cache_row_count = partial_value[2].shape[0]
    return (
        (partial_value[2] / partial_value[1][..., None])
        .astype(jnp.bfloat16)
        .reshape(cache_row_count, QUERY_HEADS * HEAD_WIDTH)
    )


def local(
    draft_node_queries,
    draft_node_keys,
    draft_node_values,
    paged_key_cache,
    paged_value_cache,
    context_length,
    parents,
    accepted_path,
    out_weight,
):
    own_rows = draft_node_queries.shape[0]
    draft_node_count = parents.shape[0]
    query_group_width = QUERY_HEADS // KEY_VALUE_HEADS
    position = lax.axis_index("blk")
    offset = position * paged_key_cache.shape[0]
    length = context_length[0]
    ancestry = ancestors(parents)
    own_ancestry = lax.dynamic_slice_in_dim(ancestry, position * own_rows, own_rows, 0)
    own_queries = draft_node_queries.reshape(
        own_rows, KEY_VALUE_HEADS, query_group_width, HEAD_WIDTH
    )
    every_query_row, keys_all, values_all = (
        lax.all_gather(draft_node_queries, "blk", axis=0, tiled=True),
        lax.all_gather(draft_node_keys, "blk", axis=0, tiled=True),
        lax.all_gather(draft_node_values, "blk", axis=0, tiled=True),
    )
    grouped_queries = every_query_row.reshape(
        draft_node_count, KEY_VALUE_HEADS, query_group_width, HEAD_WIDTH
    )
    partial_value = cache_partial(
        grouped_queries,
        paged_key_cache,
        paged_value_cache,
        offset,
        length,
        fresh_state(draft_node_count),
    )
    arrived = (
        lax.all_to_all(partial_value[0][None], "blk", split_axis=1, concat_axis=0, tiled=True),
        lax.all_to_all(partial_value[1][None], "blk", split_axis=1, concat_axis=0, tiled=True),
        lax.all_to_all(partial_value[2][None], "blk", split_axis=1, concat_axis=0, tiled=True),
    )
    maxima = jnp.max(arrived[0], axis=0)
    scales = jnp.exp(arrived[0] - maxima[None])
    totals = jnp.sum(arrived[1] * scales, axis=0)
    weighted = jnp.sum(arrived[2] * scales[..., None], axis=0)
    partial_value = combine(
        (maxima, totals, weighted), tree_partial(own_queries, keys_all, values_all, own_ancestry)
    )
    attention_own = normalize(partial_value)
    attention_all = lax.all_gather(attention_own, "blk", axis=0, tiled=True)
    picker = (
        accepted_path[:, None] == jnp.arange(draft_node_count, dtype=jnp.int32)[None, :]
    ).astype(jnp.bfloat16)
    path_rows = jnp.dot(picker, attention_all, preferred_element_type=jnp.float32).astype(
        jnp.bfloat16
    )
    path_output = lax.dot_general(
        path_rows, out_weight, (((1,), (1,)), ((), ())), preferred_element_type=jnp.float32
    ).astype(jnp.bfloat16)
    return (attention_own, path_output)


def solution(mesh):
    in_specs = (
        P(("req", "blk"), None),
        P(("req", "blk"), None),
        P(("req", "blk"), None),
        P(("req", "blk"), None),
        P(("req", "blk"), None),
        P("req"),
        P("req"),
        P("req"),
        P("blk", None),
    )
    out_specs = (P(("req", "blk"), None), P("req", "blk"))
    return jax.shard_map(local, mesh=mesh, in_specs=in_specs, out_specs=out_specs, check_vma=False)
```

profile of v0, /device:TPU:0, one launch (start us, length us, event | category | flops | bytes accessed | tf_op | source)
XLA Modules:
  0.0 78.9 jit_solution(13678298688536361862)
XLA Ops:
  1.3 10.8 %all_gather.12 = bf16[32,4096]{1,0:T(8,128)(2,1)S(1)} all-gather(bf16[8,4096]{1,0:T(8,128)(2,1)} %param.9), channel_id=1, replica_groups=mesh['req'=8,'blk'=4] {'blk'}, dimensions={0}, use_global_device_ids=true | all-gather | bytes 327680 | tf_op jit(solution)/shard_map/all_gather | solution.py:127
  12.0 0.5 reshape.137
  12.6 1.3 %copy.73 = bf16[512,512]{0,1:T(8,128)(2,1)S(1)} copy(bf16[512,512]{1,0:T(8,128)(2,1)} %param.12) | data formatting | bytes 1048576 | tf_op args[3]
  13.9 0.9 %bitcast_reduce_fusion = (f32[32,8,8]{0,2,1:T(8,128)S(1)}, f32[8,512,32,8]{1,2,3,0:T(8,128)S(1)}) fusion(pred[512]{0:T(512)(128)(4,1)S(1)} %add_compare_fusion, bf16[512,8,64,1]{0,2,3,1:T(8,128)(2,1)S(1)} %bitcast.85, bf16[32,8,8,64]{3,2,1,0:T(8,128)(2,1)S(1)} %reshape.137), kind=kOutput, calls=%fused_computation.2 | convolution fusion | flops 137361408 | bytes 4989440 | tf_op jit(solution)/shard_map/while/body/eval_jaxpr/mrjz,xrz->mrjx/dot_general | solution.py:49
  14.8 1.4 %fusion.2 = (f32[32,8,8]{0,2,1:T(8,128)S(1)}, bf16[32,8,8,512]{3,0,2,1:T(8,128)(2,1)S(1)}) fusion(f32[8,512,32,8]{1,2,3,0:T(8,128)S(1)} %get-tuple-element.41, f32[32,8,8]{0,2,1:T(8,128)S(1)} %get-tuple-element.39, pred[512]{0:T(512)(128)(4,1)S(1)} %add_compare_fusion), kind=kLoop, calls=%fused_computation.6 | loop fusion | flops 6289408 | bytes 6308352 | tf_op jit(solution)/shard_map/while/body/eval_jaxpr/reduce_sum | solution.py:56
  16.4 0.7 reshape.151
  17.1 3.2 %all-to-all-start.2 = ((f32[4,1,512]{2,1,0:T(1,128)}), f32[4,1,512]{2,1,0:T(1,128)S(1)}, u32[]{:S(2)}, u32[]{:S(2)}) async-start(f32[4,1,512]{2,1,0:T(1,128)} %reshape.151), calls=%async_computation.2 | async-start | bytes 16384 | tf_op jit(solution)/shard_map/all_to_all | solution.py:144
  21.7 8.7 %all_gather.13 = bf16[32,512]{1,0:T(8,128)(2,1)S(1)} all-gather(bf16[8,512]{1,0:T(8,128)(2,1)S(1)} %copy-done.3), channel_id=1, replica_groups=mesh['req'=8,'blk'=4] {'blk'}, dimensions={0}, use_global_device_ids=true | all-gather | bytes 40960 | tf_op jit(solution)/shard_map/all_gather | solution.py:128
  30.9 0.8 copy.75
  31.7 1.0 %copy.76 = bf16[512,512]{0,1:T(8,128)(2,1)} copy(bf16[512,512]{1,0:T(8,128)(2,1)S(1)} %copy-done) | data formatting | bytes 1048576 | tf_op args[4]
  32.7 2.4 %fusion.12 = f32[1,32,8,8,64]{4,3,1,2,0:T(8,128)S(1)} fusion(bf16[512,8,64,1]{0,2,3,1:T(8,128)(2,1)} %bitcast.91, bf16[32,8,8,512]{3,0,2,1:T(8,128)(2,1)S(1)} %get-tuple-element.26, f32[32,8,8]{2,0,1:T(8,128)} %copy.75), kind=kOutput, calls=%fused_computation.12 | convolution fusion | flops 134348800 | bytes 3153920 | tf_op jit(solution)/shard_map/while/body/eval_jaxpr/zvle,evt->zvlt/dot_general | solution.py:57
  35.5 0.7 reshape.149
  36.4 1.4 %reshape.147 = f32[4,1,32768]{2,1,0:T(1,128)} reshape(f32[32,1,8,8,64]{4,3,2,1,0:T(8,128)S(1)} %bitcast.84) | data formatting | bytes 1048576
  37.9 3.2 %all-to-all-start.1 = ((f32[4,1,512]{2,1,0:T(1,128)}), f32[4,1,512]{2,1,0:T(1,128)S(1)}, u32[]{:S(2)}, u32[]{:S(2)}) async-start(f32[4,1,512]{2,1,0:T(1,128)} %reshape.149), calls=%async_computation.1 | async-start | bytes 16384 | tf_op jit(solution)/shard_map/all_to_all | solution.py:143
  41.1 8.6 %all_gather.14 = bf16[32,512]{1,0:T(8,128)(2,1)S(1)} all-gather(bf16[8,512]{1,0:T(8,128)(2,1)S(1)} %copy-done.4), channel_id=1, replica_groups=mesh['req'=8,'blk'=4] {'blk'}, dimensions={0}, use_global_device_ids=true | all-gather | bytes 40960 | tf_op jit(solution)/shard_map/all_gather | solution.py:129
  49.9 0.5 broadcast.122
  50.4 0.7 reduce.1
  51.2 3.5 %all-to-all-start = ((f32[4,1,32768]{2,1,0:T(1,128)}), f32[4,1,32768]{2,1,0:T(1,128)S(1)}, u32[]{:S(2)}, u32[]{:S(2)}) async-start(f32[4,1,32768]{2,1,0:T(1,128)} %reshape.147), calls=%async_computation | async-start | bytes 1048576 | tf_op jit(solution)/shard_map/all_to_all | solution.py:145
  54.7 0.7 reduce.2
  56.0 5.2 %all-to-all-done = f32[4,1,32768]{2,1,0:T(1,128)S(1)} async-done(((f32[4,1,32768]{2,1,0:T(1,128)}), f32[4,1,32768]{2,1,0:T(1,128)S(1)}, u32[]{:S(2)}, u32[]{:S(2)}) %all-to-all-start) | async-done | bytes 524320 | tf_op jit(solution)/shard_map/all_to_all | solution.py:145
  61.2 2.1 %reduce = f32[4,32768]{1,0:T(4,128)S(1)} reduce(f32[4,1,32768]{2,1,0:T(1,128)S(1)} %all-to-all-done, f32[]{:T(128)} %broadcast.122), dimensions={1}, to_apply=%all_to_all.12.reduce_sub_computation | reduce | bytes 1048580 | tf_op jit(solution)/shard_map/all_to_all | solution.py:145
  63.4 0.5 reshape.148
  64.9 9.0 %all_gather.15 = bf16[32,4096]{1,0:T(8,128)(2,1)S(1)} all-gather(bf16[8,4096]{1,0:T(8,128)(2,1)S(1)} %reshape.142), channel_id=1, replica_groups=mesh['req'=8,'blk'=4] {'blk'}, dimensions={0}, use_global_device_ids=true | all-gather | bytes 327680 | tf_op jit(solution)/shard_map/all_gather | solution.py:155
  73.9 5.0 %fusion.23 = bf16[8,720]{1,0:T(8,128)(2,1)} fusion(bf16[720,4096]{1,0:T(8,128)(2,1)} %param.17, bf16[32,4096]{1,0:T(8,128)(2,1)S(1)} %all_gather.15, s32[8]{0:T(128)S(1)} %copy-done.5), kind=kOutput, calls=%fused_computation.23 | convolution fusion | flops 49321856 | bytes 6171936 | tf_op jit(solution)/shard_map/dot_general | solution.py:162
  (55 shorter events, 4.4 us)
Async XLA Ops:
  14.8 5.6 %copy-start.1 = (bf16[8,4096]{1,0:T(8,128)(2,1)S(1)}, bf16[8,4096]{1,0:T(8,128)(2,1)}, u32[]{:S(2)}) copy-start(bf16[8,4096]{1,0:T(8,128)(2,1)} %param.9) | copy-start | bytes 196612
  14.8 5.8 %copy-start.6 = (s32[32]{0:T(128)S(1)}, s32[32]{0:T(128)}, u32[]{:S(2)}) copy-start(s32[32]{0:T(128)} %param.15) | copy-start | bytes 388
  14.8 6.9 %copy-start.3 = (bf16[8,512]{1,0:T(8,128)(2,1)S(1)}, bf16[8,512]{1,0:T(8,128)(2,1)}, u32[]{:S(2)}) copy-start(bf16[8,512]{1,0:T(8,128)(2,1)} %param.10) | copy-start | bytes 24580
  14.8 16.9 %copy-start = (bf16[512,512]{1,0:T(8,128)(2,1)S(1)}, bf16[512,512]{1,0:T(8,128)(2,1)}, u32[]{:S(2)}) copy-start(bf16[512,512]{1,0:T(8,128)(2,1)} %param.13) | copy-start | bytes 1572868
  17.1 20.8 %all-to-all-start.2 = ((f32[4,1,512]{2,1,0:T(1,128)}), f32[4,1,512]{2,1,0:T(1,128)S(1)}, u32[]{:S(2)}, u32[]{:S(2)}) async-start(f32[4,1,512]{2,1,0:T(1,128)} %reshape.151), calls=%async_computation.2 | async-start | bytes 16384 | tf_op jit(solution)/shard_map/all_to_all | solution.py:144
  32.7 8.5 %copy-start.4 = (bf16[8,512]{1,0:T(8,128)(2,1)S(1)}, bf16[8,512]{1,0:T(8,128)(2,1)}, u32[]{:S(2)}) copy-start(bf16[8,512]{1,0:T(8,128)(2,1)} %param.11) | copy-start | bytes 24580
  37.9 13.3 %all-to-all-start.1 = ((f32[4,1,512]{2,1,0:T(1,128)}), f32[4,1,512]{2,1,0:T(1,128)S(1)}, u32[]{:S(2)}, u32[]{:S(2)}) async-start(f32[4,1,512]{2,1,0:T(1,128)} %reshape.149), calls=%async_computation.1 | async-start | bytes 16384 | tf_op jit(solution)/shard_map/all_to_all | solution.py:143
  51.2 10.0 %all-to-all-start = ((f32[4,1,32768]{2,1,0:T(1,128)}), f32[4,1,32768]{2,1,0:T(1,128)S(1)}, u32[]{:S(2)}, u32[]{:S(2)}) async-start(f32[4,1,32768]{2,1,0:T(1,128)} %reshape.147), calls=%async_computation | async-start | bytes 1048576 | tf_op jit(solution)/shard_map/all_to_all | solution.py:145
  55.6 18.3 %copy-start.5 = (s32[8]{0:T(128)S(1)}, s32[8]{0:T(128)}, u32[]{:S(2)}) copy-start(s32[8]{0:T(128)} %param.16) | copy-start | bytes 100
  64.9 14.0 %copy-start.2 = (bf16[8,4096]{1,0:T(8,128)(2,1)}, bf16[8,4096]{1,0:T(8,128)(2,1)S(1)}, u32[]{:S(2)}) copy-start(bf16[8,4096]{1,0:T(8,128)(2,1)S(1)} %reshape.142) | copy-start | bytes 196612
where the time goes:
time: 79.5 us; the launch traced here: 78.9 us
  blocking collectives  37 us (47%)
  matrix products  10.1 us (13%)
  starting transfers between devices  9.98 us (13%)
  local copies, waits for them, and re-layouts  9.31 us (12%)
  other arithmetic  5.63 us (7%)
  waiting for transfers between devices  5.21 us (7%)
  between operations  1.63 us (2%)
    all_gather x1, blocking collectives, local(): lax.all_gather(draft_node_queries, 'blk', axis=0, tiled=True)  10.8 us
    all_gather x1, blocking collectives, local(): attention_all = lax.all_gather(attention_own, 'blk', axis=0, tiled=True)  8.98 us
    all_gather x1, blocking collectives, local(): lax.all_gather(draft_node_keys, 'blk', axis=0, tiled=True)  8.65 us
    all_gather x1, blocking collectives, local(): lax.all_gather(draft_node_values, 'blk', axis=0, tiled=True)  8.64 us
    unnamed x24, local copies, waits for them, and re-layouts  6.08 us
    all_to_all x1, waiting for transfers between devices, local(): lax.all_to_all(partial_value[2][None], 'blk', split_axis=1, concat_axis=0...  5.21 us
    dot_general x1, matrix products, local(): lax.dot_general(path_rows, out_weight, (((1,), (1,)), ((), ())), preferre...  5.04 us
    all_to_all x1, starting transfers between devices, local(): lax.all_to_all(partial_value[2][None], 'blk', split_axis=1, concat_axis=0...  3.48 us
  transfers between devices with their start and end apart: 3, of which 1 were waited for; matrix products, arithmetic and copies ran while one was open for 14% of the time, Pallas kernels for 0%

commit v1 on v0

--- a/solution.py
+++ b/solution.py
@@ -7,6 +7,17 @@
 KEY_VALUE_HEADS = 8
 HEAD_WIDTH = 64
 score_after_mask = -1e30
+
+
+def around_the_ring(block, mesh_axis, dim):
+    size = lax.axis_size(mesh_axis)
+    right = [(i, (i + 1) % size) for i in range(size)]
+    parts = [block]
+    for far in range(1, size):
+        parts = [lax.ppermute(parts[0], mesh_axis, right), *parts]
+    full = jnp.concatenate(parts, axis=dim)
+    shift = (lax.axis_index(mesh_axis) + 1) * parts[-1].shape[dim]
+    return jnp.roll(full, shift, axis=dim)
 
 
 def ancestors(parents):
@@ -152,7 +163,7 @@
         (maxima, totals, weighted), tree_partial(own_queries, keys_all, values_all, own_ancestry)
     )
     attention_own = normalize(partial_value)
-    attention_all = lax.all_gather(attention_own, "blk", axis=0, tiled=True)
+    attention_all = around_the_ring(attention_own, "blk", 0)
     picker = (
         accepted_path[:, None] == jnp.arange(draft_node_count, dtype=jnp.int32)[None, :]
     ).astype(jnp.bfloat16)

time: 79.5 us -> 86.9 us (1.093)
  waiting for transfers between devices: 5.21 us -> 18.9 us
  blocking collectives: 37 us -> 28 us
  starting transfers between devices: 9.98 us -> 12.6 us
    ppermute x0 -> x3, waiting for transfers between devices: none -> 13.5 us  [around_the_ring(): parts = [lax.ppermute(parts[0], mesh_axis, right), *parts]]
    all_gather x1 -> x0, blocking collectives: 8.98 us -> none  [local(): attention_all = lax.all_gather(attention_own, 'blk', axis=0, tiled=True)]
    ppermute x0 -> x3, starting transfers between devices: none -> 2.58 us  [around_the_ring(): parts = [lax.ppermute(parts[0], mesh_axis, right), *parts]]
    unnamed x24 -> x31, local copies, waits for them, and re-layouts: 6.08 us -> 6.13 us
  transfers between devices with their start and end apart: 3 -> 6, of which waited for: 1 -> 4; matrix products, arithmetic and copies ran while one was open for 14% -> 13% of each run, Pallas kernels for 0% -> 0%
where the time goes in v1:
time: 86.9 us; the launch traced here: 86.3 us
  blocking collectives  28 us (32%)
  waiting for transfers between devices  18.9 us (22%)
  starting transfers between devices  12.6 us (14%)
  matrix products  10.1 us (12%)
  local copies, waits for them, and re-layouts  9.37 us (11%)
  other arithmetic  5.63 us (6%)
  between operations  1.7 us (2%)
    ppermute x3, waiting for transfers between devices, around_the_ring(): parts = [lax.ppermute(parts[0], mesh_axis, right), *parts]  13.5 us
    all_gather x1, blocking collectives, local(): lax.all_gather(draft_node_queries, 'blk', axis=0, tiled=True)  10.8 us
    all_gather x1, blocking collectives, local(): lax.all_gather(draft_node_keys, 'blk', axis=0, tiled=True)  8.65 us
    all_gather x1, blocking collectives, local(): lax.all_gather(draft_node_values, 'blk', axis=0, tiled=True)  8.64 us
    unnamed x31, local copies, waits for them, and re-layouts  6.13 us
    all_to_all x1, waiting for transfers between devices, local(): lax.all_to_all(partial_value[2][None], 'blk', split_axis=1, concat_axis=0...  5.38 us
    dot_general x1, matrix products, local(): lax.dot_general(path_rows, out_weight, (((1,), (1,)), ((), ())), preferre...  5.05 us
    all_to_all x1, starting transfers between devices, local(): lax.all_to_all(partial_value[2][None], 'blk', split_axis=1, concat_axis=0...  3.48 us
  transfers between devices with their start and end apart: 6, of which 4 were waited for; matrix products, arithmetic and copies ran while one was open for 13% of the time, Pallas kernels for 0%

profile of v1, /device:TPU:0, one launch (start us, length us, event | category | flops | bytes accessed | tf_op | source)
XLA Modules:
  0.0 86.3 jit_solution(14992059178439946525)
XLA Ops:
  1.3 10.8 %all_gather.9 = bf16[32,4096]{1,0:T(8,128)(2,1)S(1)} all-gather(bf16[8,4096]{1,0:T(8,128)(2,1)} %param.9), channel_id=1, replica_groups=mesh['req'=8,'blk'=4] {'blk'}, dimensions={0}, use_global_device_ids=true | all-gather | bytes 327680 | tf_op jit(solution)/shard_map/all_gather | solution.py:138
  12.6 1.3 %copy.73 = bf16[512,512]{0,1:T(8,128)(2,1)S(1)} copy(bf16[512,512]{1,0:T(8,128)(2,1)} %param.12) | data formatting | bytes 1048576 | tf_op args[3]
  13.9 0.9 %bitcast_reduce_fusion = (f32[32,8,8]{0,2,1:T(8,128)S(1)}, f32[8,512,32,8]{1,2,3,0:T(8,128)S(1)}) fusion(pred[512]{0:T(512)(128)(4,1)S(1)} %add_compare_fusion, bf16[512,8,64,1]{0,2,3,1:T(8,128)(2,1)S(1)} %bitcast.84, bf16[32,8,8,64]{3,2,1,0:T(8,128)(2,1)S(1)} %reshape.137), kind=kOutput, calls=%fused_computation.2 | convolution fusion | flops 137361408 | bytes 4989440 | tf_op jit(solution)/shard_map/while/body/eval_jaxpr/mrjz,xrz->mrjx/dot_general | solution.py:60
  14.8 1.4 %fusion.2 = (f32[32,8,8]{0,2,1:T(8,128)S(1)}, bf16[32,8,8,512]{3,0,2,1:T(8,128)(2,1)S(1)}) fusion(f32[8,512,32,8]{1,2,3,0:T(8,128)S(1)} %get-tuple-element.41, f32[32,8,8]{0,2,1:T(8,128)S(1)} %get-tuple-element.39, pred[512]{0:T(512)(128)(4,1)S(1)} %add_compare_fusion), kind=kLoop, calls=%fused_computation.6 | loop fusion | flops 6289408 | bytes 6308352 | tf_op jit(solution)/shard_map/while/body/eval_jaxpr/reduce_sum | solution.py:67
  16.4 0.7 reshape.151
  17.1 3.2 %all-to-all-start.2 = ((f32[4,1,512]{2,1,0:T(1,128)}), f32[4,1,512]{2,1,0:T(1,128)S(1)}, u32[]{:S(2)}, u32[]{:S(2)}) async-start(f32[4,1,512]{2,1,0:T(1,128)} %reshape.151), calls=%async_computation.2 | async-start | bytes 16384 | tf_op jit(solution)/shard_map/all_to_all | solution.py:155
  21.7 8.7 %all_gather.10 = bf16[32,512]{1,0:T(8,128)(2,1)S(1)} all-gather(bf16[8,512]{1,0:T(8,128)(2,1)S(1)} %copy-done.3), channel_id=1, replica_groups=mesh['req'=8,'blk'=4] {'blk'}, dimensions={0}, use_global_device_ids=true | all-gather | bytes 40960 | tf_op jit(solution)/shard_map/all_gather | solution.py:139
  30.9 0.8 copy.75
  31.7 1.0 %copy.76 = bf16[512,512]{0,1:T(8,128)(2,1)} copy(bf16[512,512]{1,0:T(8,128)(2,1)S(1)} %copy-done.1) | data formatting | bytes 1048576 | tf_op args[4]
  32.7 2.4 %fusion.12 = f32[1,32,8,8,64]{4,3,1,2,0:T(8,128)S(1)} fusion(bf16[512,8,64,1]{0,2,3,1:T(8,128)(2,1)} %bitcast.90, bf16[32,8,8,512]{3,0,2,1:T(8,128)(2,1)S(1)} %get-tuple-element.26, f32[32,8,8]{2,0,1:T(8,128)} %copy.75), kind=kOutput, calls=%fused_computation.12 | convolution fusion | flops 134348800 | bytes 3153920 | tf_op jit(solution)/shard_map/while/body/eval_jaxpr/zvle,evt->zvlt/dot_general | solution.py:68
  35.6 0.7 reshape.149
  36.4 1.4 %reshape.147 = f32[4,1,32768]{2,1,0:T(1,128)} reshape(f32[32,1,8,8,64]{4,3,2,1,0:T(8,128)S(1)} %bitcast.83) | data formatting | bytes 1048576
  37.9 3.2 %all-to-all-start.1 = ((f32[4,1,512]{2,1,0:T(1,128)}), f32[4,1,512]{2,1,0:T(1,128)S(1)}, u32[]{:S(2)}, u32[]{:S(2)}) async-start(f32[4,1,512]{2,1,0:T(1,128)} %reshape.149), calls=%async_computation.1 | async-start | bytes 16384 | tf_op jit(solution)/shard_map/all_to_all | solution.py:154
  41.1 8.6 %all_gather.11 = bf16[32,512]{1,0:T(8,128)(2,1)S(1)} all-gather(bf16[8,512]{1,0:T(8,128)(2,1)S(1)} %copy-done.4), channel_id=1, replica_groups=mesh['req'=8,'blk'=4] {'blk'}, dimensions={0}, use_global_device_ids=true | all-gather | bytes 40960 | tf_op jit(solution)/shard_map/all_gather | solution.py:140
  50.4 0.7 reduce.1
  51.2 3.5 %all-to-all-start = ((f32[4,1,32768]{2,1,0:T(1,128)}), f32[4,1,32768]{2,1,0:T(1,128)S(1)}, u32[]{:S(2)}, u32[]{:S(2)}) async-start(f32[4,1,32768]{2,1,0:T(1,128)} %reshape.147), calls=%async_computation | async-start | bytes 1048576 | tf_op jit(solution)/shard_map/all_to_all | solution.py:156
  54.7 0.7 reduce.2
  56.0 5.4 %all-to-all-done = f32[4,1,32768]{2,1,0:T(1,128)S(1)} async-done(((f32[4,1,32768]{2,1,0:T(1,128)}), f32[4,1,32768]{2,1,0:T(1,128)S(1)}, u32[]{:S(2)}, u32[]{:S(2)}) %all-to-all-start) | async-done | bytes 524320 | tf_op jit(solution)/shard_map/all_to_all | solution.py:156
  61.4 2.1 %reduce = f32[4,32768]{1,0:T(4,128)S(1)} reduce(f32[4,1,32768]{2,1,0:T(1,128)S(1)} %all-to-all-done, f32[]{:T(128)} %broadcast.123), dimensions={1}, to_apply=%all_to_all.12.reduce_sub_computation | reduce | bytes 1048580 | tf_op jit(solution)/shard_map/all_to_all | solution.py:156
  65.1 2.0 %collective-permute-start = (bf16[8,4096]{1,0:T(8,128)(2,1)S(1)}, bf16[8,4096]{1,0:T(8,128)(2,1)S(1)}, u32[]{:S(2)}, u32[]{:S(2)}) collective-permute-start(bf16[8,4096]{1,0:T(8,128)(2,1)S(1)} %reshape.142), channel_id=1, source_target_pairs={{0,1},{1,2},{2,3},{3,0},{4,5},{5,6},{6,7},{7,4},{8,9},{9,10},{10,1... | collective-permute-start | bytes 196616 | tf_op jit(solution)/shard_map/ppermute | solution.py:17
  67.1 3.7 %collective-permute-done = bf16[8,4096]{1,0:T(8,128)(2,1)S(1)} collective-permute-done((bf16[8,4096]{1,0:T(8,128)(2,1)S(1)}, bf16[8,4096]{1,0:T(8,128)(2,1)S(1)}, u32[]{:S(2)}, u32[]{:S(2)}) %collective-permute-start) | collective-permute-done | bytes 65568 | tf_op jit(solution)/shard_map/ppermute | solution.py:17
  71.4 4.6 %collective-permute-done.1 = bf16[8,4096]{1,0:T(8,128)(2,1)S(1)} collective-permute-done((bf16[8,4096]{1,0:T(8,128)(2,1)S(1)}, bf16[8,4096]{1,0:T(8,128)(2,1)S(1)}, u32[]{:S(2)}, u32[]{:S(2)}) %collective-permute-start.1) | collective-permute-done | bytes 65568 | tf_op jit(solution)/shard_map/ppermute | solution.py:17
  76.0 5.2 %collective-permute-done.2 = bf16[8,4096]{1,0:T(8,128)(2,1)S(1)} collective-permute-done((bf16[8,4096]{1,0:T(8,128)(2,1)S(1)}, bf16[8,4096]{1,0:T(8,128)(2,1)S(1)}, u32[]{:S(2)}, u32[]{:S(2)}) %collective-permute-start.2) | collective-permute-done | bytes 65568 | tf_op jit(solution)/shard_map/ppermute | solution.py:17
  81.3 5.0 %fusion.23 = bf16[8,720]{1,0:T(8,128)(2,1)} fusion(bf16[720,4096]{1,0:T(8,128)(2,1)} %param.17, bf16[64,4096]{1,0:T(8,128)(2,1)S(1)} %constant_dynamic-update-slice_fusion, s32[]{:T(128)S(6)} %select_n.42, s32[8]{0:T(128)S(1)} %copy-done.5), kind=kOutput, calls=%fused_computation.23 | convolution fusion | flops 49321856 | bytes 6172420 | tf_op jit(solution)/shard_map/dot_general | solution.py:173
  (68 shorter events, 6.6 us)
Async XLA Ops:
  14.8 5.6 %copy-start.2 = (bf16[8,4096]{1,0:T(8,128)(2,1)S(1)}, bf16[8,4096]{1,0:T(8,128)(2,1)}, u32[]{:S(2)}) copy-start(bf16[8,4096]{1,0:T(8,128)(2,1)} %param.9) | copy-start | bytes 196612
  14.8 5.8 %copy-start.6 = (s32[32]{0:T(128)S(1)}, s32[32]{0:T(128)}, u32[]{:S(2)}) copy-start(s32[32]{0:T(128)} %param.15) | copy-start | bytes 388
  14.8 6.9 %copy-start.3 = (bf16[8,512]{1,0:T(8,128)(2,1)S(1)}, bf16[8,512]{1,0:T(8,128)(2,1)}, u32[]{:S(2)}) copy-start(bf16[8,512]{1,0:T(8,128)(2,1)} %param.10) | copy-start | bytes 24580
  14.8 16.9 %copy-start.1 = (bf16[512,512]{1,0:T(8,128)(2,1)S(1)}, bf16[512,512]{1,0:T(8,128)(2,1)}, u32[]{:S(2)}) copy-start(bf16[512,512]{1,0:T(8,128)(2,1)} %param.13) | copy-start | bytes 1572868
  17.1 20.8 %all-to-all-start.2 = ((f32[4,1,512]{2,1,0:T(1,128)}), f32[4,1,512]{2,1,0:T(1,128)S(1)}, u32[]{:S(2)}, u32[]{:S(2)}) async-start(f32[4,1,512]{2,1,0:T(1,128)} %reshape.151), calls=%async_computation.2 | async-start | bytes 16384 | tf_op jit(solution)/shard_map/all_to_all | solution.py:155
  32.7 8.5 %copy-start.4 = (bf16[8,512]{1,0:T(8,128)(2,1)S(1)}, bf16[8,512]{1,0:T(8,128)(2,1)}, u32[]{:S(2)}) copy-start(bf16[8,512]{1,0:T(8,128)(2,1)} %param.11) | copy-start | bytes 24580
  37.9 13.3 %all-to-all-start.1 = ((f32[4,1,512]{2,1,0:T(1,128)}), f32[4,1,512]{2,1,0:T(1,128)S(1)}, u32[]{:S(2)}, u32[]{:S(2)}) async-start(f32[4,1,512]{2,1,0:T(1,128)} %reshape.149), calls=%async_computation.1 | async-start | bytes 16384 | tf_op jit(solution)/shard_map/all_to_all | solution.py:154
  51.2 10.2 %all-to-all-start = ((f32[4,1,32768]{2,1,0:T(1,128)}), f32[4,1,32768]{2,1,0:T(1,128)S(1)}, u32[]{:S(2)}, u32[]{:S(2)}) async-start(f32[4,1,32768]{2,1,0:T(1,128)} %reshape.147), calls=%async_computation | async-start | bytes 1048576 | tf_op jit(solution)/shard_map/all_to_all | solution.py:156
  55.7 25.5 %copy-start.5 = (s32[8]{0:T(128)S(1)}, s32[8]{0:T(128)}, u32[]{:S(2)}) copy-start(s32[8]{0:T(128)} %param.16) | copy-start | bytes 100
  65.1 21.3 %copy-start = (bf16[8,4096]{1,0:T(8,128)(2,1)}, bf16[8,4096]{1,0:T(8,128)(2,1)S(1)}, u32[]{:S(2)}) copy-start(bf16[8,4096]{1,0:T(8,128)(2,1)S(1)} %reshape.142) | copy-start | bytes 196612
  65.1 5.7 %collective-permute-start = (bf16[8,4096]{1,0:T(8,128)(2,1)S(1)}, bf16[8,4096]{1,0:T(8,128)(2,1)S(1)}, u32[]{:S(2)}, u32[]{:S(2)}) collective-permute-start(bf16[8,4096]{1,0:T(8,128)(2,1)S(1)} %reshape.142), channel_id=1, source_target_pairs={{0,1},{1,2},{2,3},{3,0},{4,5},{5,6},{6,7},{7,4},{8,9},{9,10},{10,1... | collective-permute-start | bytes 196616 | tf_op jit(solution)/shard_map/ppermute | solution.py:17
  70.8 5.2 %collective-permute-start.1 = (bf16[8,4096]{1,0:T(8,128)(2,1)S(1)}, bf16[8,4096]{1,0:T(8,128)(2,1)S(1)}, u32[]{:S(2)}, u32[]{:S(2)}) collective-permute-start(bf16[8,4096]{1,0:T(8,128)(2,1)S(1)} %collective-permute-done), channel_id=1, source_target_pairs={{0,1},{1,2},{2,3},{3,0},{4,5},{5,6},{6,7},{7,4},{8,9},{9,10},{10,1... | collective-permute-start | bytes 196616 | tf_op jit(solution)/shard_map/ppermute | solution.py:17
  76.0 5.2 %collective-permute-start.2 = (bf16[8,4096]{1,0:T(8,128)(2,1)S(1)}, bf16[8,4096]{1,0:T(8,128)(2,1)S(1)}, u32[]{:S(2)}, u32[]{:S(2)}) collective-permute-start(bf16[8,4096]{1,0:T(8,128)(2,1)S(1)} %collective-permute-done.1), channel_id=1, source_target_pairs={{0,1},{1,2},{2,3},{3,0},{4,5},{5,6},{6,7},{7,4},{8,9},{9,10},{10,1... | collective-permute-start | bytes 196616 | tf_op jit(solution)/shard_map/ppermute | solution.py:17
